TPU v7x, 256 devices: a whole 4x4x8 slice. The times are simulated.
256 devices in a mesh: gx: 8 (over z_hi, core), gy: 4 (over y), gz: 8 (over z_lo, x).
Axes of the slice: x: 4, y: 4, z: 8 (z_hi: 4, z_lo: 2; z = z_hi * 2 + z_lo), core: 2. Of those that a mesh axis runs over, the one named last changes fastest.
Arguments:
- field: float32 [256, 1024, 512], P('gz', 'gx', 'gy'), may hold values from -48 to 48
- factor_a: float32 [1024, 1024], replicated, may hold values from -0.5 to 3.5
- factor_b: float32 [512, 512], replicated, may hold values from -0.5 to 3.5
- factor_c: float32 [256, 256], replicated, may hold values from -0.5 to 3.5
Outputs:
- propagated: float32 [256, 1024, 512], P('gz', 'gx', 'gy')
All inputs are finite; a program needn't handle non-finite values.
Results may differ from a plain program's by a relative error of at most 0.00007.
Values sent between devices are 32-bit elements; how exact they have to be, the bound alone decides.
No kernel may reach another device: no remote copies, remote signals or barrier semaphores. Data moves between devices by JAX's collectives and lax.ppermute only.
A program may use at most 64 MiB of HBM per device.

v0:
```python
import jax
import jax.numpy as jnp
from jax import lax
from jax.sharding import Mesh
from jax.sharding import PartitionSpec as P

GX = ("gx_0", "gx_1")
GX_GY = ("gx_0", "gx_1", "gy")
GZ = ("gz_0", "gz_1")
GX_GY_GZ = ("gx_0", "gx_1", "gy", "gz_0", "gz_1")
epsilon = 1e-06
target_ratio = 0.5


def split_up(value, dim, size):
    dims = value.shape
    tiles = value.reshape(*dims[:dim], size, dims[dim] // size, *dims[dim + 1 :])
    return jnp.moveaxis(tiles, dim, 0)


def laid_out(tiles, dim):
    dims = list(tiles.shape[1:])
    dims[dim] *= tiles.shape[0]
    return jnp.moveaxis(tiles, 0, dim).reshape(dims)


def joined_exchange(value, axis, axes, splits, concats):
    sizes = [lax.axis_size(a) for a in axes]
    tiles = split_up(value, splits[0], sizes[0])
    tiles = jnp.moveaxis(split_up(tiles, splits[1] + 1, sizes[1]), 0, 1)
    inside = tiles.shape[2:]
    tiles = tiles.reshape(-1, *inside)
    tiles = lax.all_to_all(tiles, axis, split_axis=0, concat_axis=0, tiled=True)
    tiles = laid_out(tiles.reshape(*sizes, *inside), concats[0] + 1)
    return laid_out(tiles, concats[1])


def over_axes(value, axes):
    for axis in axes:
        value = lax.psum(value, axis)
    return value


def on_device(field, factor_a, factor_b, factor_c):
    highest = lax.Precision.HIGHEST
    count_x = lax.axis_size(GX)
    count_y = lax.axis_size("gy")

    def slab_products(slabs):
        along_one = jnp.einsum("ip,mpj->mij", factor_a, slabs, precision=highest)
        along_two = jnp.einsum("mip,jp->mij", slabs, factor_b, precision=highest)
        return along_one + along_two

    def plane_terms(tensor):
        depth_home, width_one, width_two = tensor.shape
        depth = depth_home // (count_x * count_y)
        slabs = joined_exchange(tensor, GX_GY, (GX, "gy"), (0, 0), (1, 2))
        products = slab_products(slabs)
        returned = joined_exchange(products, GX_GY, (GX, "gy"), (1, 2), (0, 0))
        returned = returned.reshape(count_y, count_x, depth, width_one, width_two)
        return returned.transpose(1, 0, 2, 3, 4).reshape(depth_home, width_one, width_two)

    def fibre_product(fibres):
        flat = fibres.reshape(fibres.shape[0], -1)
        product = jnp.dot(factor_c, flat, precision=highest).reshape(fibres.shape)
        return lax.all_to_all(product, GZ, split_axis=0, concat_axis=1, tiled=True)

    def apply_block(tensor):
        planes = plane_terms(tensor)
        fibres = fibre_product(lax.all_to_all(tensor, GZ, split_axis=1, concat_axis=0, tiled=True))
        return planes + fibres

    first_term = apply_block(field)
    size_field, size_first = (
        over_axes(jnp.sum(field * field), GX_GY_GZ),
        over_axes(jnp.sum(first_term * first_term), GX_GY_GZ),
    )
    step = target_ratio * jnp.sqrt(size_field / (size_first + epsilon))
    second_term = apply_block(first_term)
    result = field - step * first_term + step * step / 2.0 * second_term
    return result


def solution(mesh):
    finer = Mesh(
        mesh.devices.reshape(4, 2, mesh.shape["gy"], 2, 4), ("gx_0", "gx_1", "gy", "gz_0", "gz_1")
    )
    in_specs = (P(GZ, GX, "gy"), P(), P(), P())
    out_specs = P(GZ, GX, "gy")
    return jax.shard_map(
        on_device, mesh=finer, in_specs=in_specs, out_specs=out_specs, check_vma=False
    )
```

profile of v0, /device:TPU:32, one launch (start us, length us, event | category | flops | bytes accessed | tf_op | source)
XLA Modules:
  0.0 407.0 jit_solution(6824693490417956613)
XLA Ops:
  0.0 2.9 copy.44
  2.9 31.4 %all_to_all.89 = f32[32,128,128]{2,0,1:T(8,128)} all-to-all(f32[32,128,128]{2,0,1:T(8,128)S(1)} %copy.44), channel_id=1, replica_groups=mesh['gx_0'=4,'gx_1'=2,'gy'=4,'gz_0'=2,'gz_1'=4] {'gz_0','gz_1'}, dimensions={1} | all-to-all | bytes 4194304 | tf_op jit(solution)/shard_map/all_to_all | solution.py:70
  34.3 10.6 %all-to-all-start = ((f32[32,1,128,128]{3,2,1,0:T(8,128)}), f32[32,1,128,128]{3,2,1,0:T(8,128)S(1)}, u32[]{:S(2)}, u32[]{:S(2)}) async-start(f32[32,1,128,128]{3,2,1,0:T(8,128)} %bitcast), calls=%async_computation | async-start | bytes 4194304 | tf_op jit(solution)/shard_map/all_to_all | solution.py:33
  49.9 3.0 copy.46
  52.9 3.5 fusion.7
  59.0 29.7 %all-to-all-done = f32[32,1,128,128]{3,2,1,0:T(8,128)S(1)} async-done(((f32[32,1,128,128]{3,2,1,0:T(8,128)}), f32[32,1,128,128]{3,2,1,0:T(8,128)S(1)}, u32[]{:S(2)}, u32[]{:S(2)}) %all-to-all-start) | async-done | bytes 2097184 | tf_op jit(solution)/shard_map/all_to_all | solution.py:33
  88.6 14.1 %all-to-all-start.3 = ((f32[256,16,128]{2,1,0:T(8,128)}), f32[256,16,128]{2,1,0:T(8,128)}, u32[]{:S(2)}, u32[]{:S(2)}) async-start(f32[256,16,128]{2,1,0:T(8,128)} %copy.47), calls=%async_computation.3 | async-start | bytes 4194304 | tf_op jit(solution)/shard_map/all_to_all | solution.py:66
  106.1 9.1 %fusion.9 = f32[512,1024]{1,0:T(8,128)S(1)} fusion(f32[1024,512]{0,1:T(8,128)S(1)} %bitcast.108, f32[1024,1024]{1,0:T(8,128)} %param.5), kind=kOutput, calls=%fused_computation.16 | convolution fusion | flops 6442450944 | bytes 8388608 | tf_op jit(solution)/shard_map/ip,mpj->mij/dot_general | solution.py:50
  115.2 3.5 fusion.4
  121.1 7.4 %all-to-all-done.3 = f32[256,16,128]{2,1,0:T(8,128)} async-done(((f32[256,16,128]{2,1,0:T(8,128)}), f32[256,16,128]{2,1,0:T(8,128)}, u32[]{:S(2)}, u32[]{:S(2)}) %all-to-all-start.3) | async-done | bytes 2097184 | tf_op jit(solution)/shard_map/all_to_all | solution.py:66
  128.5 5.0 %all-to-all-start.1 = ((f32[32,1,128,128]{3,2,1,0:T(8,128)}), f32[32,1,128,128]{3,2,1,0:T(8,128)S(1)}, u32[]{:S(2)}, u32[]{:S(2)}) async-start(f32[32,1,128,128]{3,2,1,0:T(8,128)} %bitcast.114), calls=%async_computation.1 | async-start | bytes 4194304 | tf_op jit(solution)/shard_map/all_to_all | solution.py:33
  133.5 3.2 copy.48
  136.7 48.5 %all-to-all-done.1 = f32[32,1,128,128]{3,2,1,0:T(8,128)S(1)} async-done(((f32[32,1,128,128]{3,2,1,0:T(8,128)}), f32[32,1,128,128]{3,2,1,0:T(8,128)S(1)}, u32[]{:S(2)}, u32[]{:S(2)}) %all-to-all-start.1) | async-done | bytes 2097184 | tf_op jit(solution)/shard_map/all_to_all | solution.py:33
  191.8 4.3 %all-to-all-start.6 = ((f32[32,128,128]{2,0,1:T(8,128)}), f32[32,128,128]{2,0,1:T(8,128)}, u32[]{:S(2)}, u32[]{:S(2)}) async-start(f32[32,128,128]{2,0,1:T(8,128)} %copy.53), calls=%async_computation.6 | async-start | bytes 4194304 | tf_op jit(solution)/shard_map/all_to_all | solution.py:70
  196.1 3.2 add.44
  199.3 22.3 %all-to-all-done.6 = f32[32,128,128]{2,0,1:T(8,128)} async-done(((f32[32,128,128]{2,0,1:T(8,128)}), f32[32,128,128]{2,0,1:T(8,128)}, u32[]{:S(2)}, u32[]{:S(2)}) %all-to-all-start.6) | async-done | bytes 2097184 | tf_op jit(solution)/shard_map/all_to_all | solution.py:70
  221.6 5.1 %all-to-all-start.4 = ((f32[32,1,128,128]{3,2,1,0:T(8,128)}), f32[32,1,128,128]{3,2,1,0:T(8,128)S(1)}, u32[]{:S(2)}, u32[]{:S(2)}) async-start(f32[32,1,128,128]{3,2,1,0:T(8,128)} %add.44), calls=%async_computation.4 | async-start | bytes 4194304 | tf_op jit(solution)/shard_map/all_to_all | solution.py:33
  229.5 5.0 %fusion = f32[2048,256]{1,0:T(8,128)} fusion(f32[256,256]{1,0:T(8,128)S(1)} %copy-done.3, f32[32,8,16,128]{3,2,1,0:T(8,128)S(1)} %bitcast.121), kind=kOutput, calls=%fused_computation | convolution fusion | flops 1610612736 | bytes 4456448 | tf_op jit(solution)/shard_map/dot_general | solution.py:65
  234.5 3.1 copy.55
  237.6 40.7 %all-to-all-done.4 = f32[32,1,128,128]{3,2,1,0:T(8,128)S(1)} async-done(((f32[32,1,128,128]{3,2,1,0:T(8,128)}), f32[32,1,128,128]{3,2,1,0:T(8,128)S(1)}, u32[]{:S(2)}, u32[]{:S(2)}) %all-to-all-start.4) | async-done | bytes 2097184 | tf_op jit(solution)/shard_map/all_to_all | solution.py:33
  278.3 4.3 %all-to-all-start.7 = ((f32[256,16,128]{2,1,0:T(8,128)}), f32[256,16,128]{2,1,0:T(8,128)}, u32[]{:S(2)}, u32[]{:S(2)}) async-start(f32[256,16,128]{2,1,0:T(8,128)} %copy.55), calls=%async_computation.7 | async-start | bytes 4194304 | tf_op jit(solution)/shard_map/all_to_all | solution.py:66
  285.9 9.1 %fusion.10 = f32[512,1024]{1,0:T(8,128)S(1)} fusion(f32[1024,512]{0,1:T(8,128)S(1)} %bitcast.110, f32[1024,1024]{1,0:T(8,128)} %param.5), kind=kOutput, calls=%fused_computation.17 | convolution fusion | flops 6442450944 | bytes 8388608 | tf_op jit(solution)/shard_map/ip,mpj->mij/dot_general | solution.py:50
  295.0 3.5 fusion.3
  300.9 7.2 %all-to-all-done.7 = f32[256,16,128]{2,1,0:T(8,128)} async-done(((f32[256,16,128]{2,1,0:T(8,128)}), f32[256,16,128]{2,1,0:T(8,128)}, u32[]{:S(2)}, u32[]{:S(2)}) %all-to-all-start.7) | async-done | bytes 2097184 | tf_op jit(solution)/shard_map/all_to_all | solution.py:66
  308.1 5.0 %all-to-all-start.5 = ((f32[32,1,128,128]{3,2,1,0:T(8,128)}), f32[32,1,128,128]{3,2,1,0:T(8,128)}, u32[]{:S(2)}, u32[]{:S(2)}) async-start(f32[32,1,128,128]{3,2,1,0:T(8,128)} %bitcast.30), calls=%async_computation.5 | async-start | bytes 4194304 | tf_op jit(solution)/shard_map/all_to_all | solution.py:33
  315.8 52.3 %all-reduce.2 = (f32[]{:T(128)}, f32[]{:T(128)}) all-reduce(f32[]{:T(128)} %multiply_reduce_fusion.1, f32[]{:T(128)} %get-tuple-element.15), channel_id=1, replica_groups=mesh['gx_0'=4,'gx_1'=2,'gy'=4,'gz_0'=2,'gz_1'=4] {'gx_0'}, use_global_device_ids=true, to_apply=%region_1.0 | all-reduce | flops 2 | bytes 16 | tf_op jit(solution)/shard_map/psum | solution.py:40
  368.1 3.2 all-reduce.4
  371.3 10.9 %all-reduce.1 = (f32[]{:T(128)}, f32[]{:T(128)}) all-reduce(f32[]{:T(128)} %get-tuple-element.13, f32[]{:T(128)} %get-tuple-element.14), channel_id=1, replica_groups=mesh['gx_0'=4,'gx_1'=2,'gy'=4,'gz_0'=2,'gz_1'=4] {'gy'}, use_global_device_ids=true, to_apply=%region_3.0 | all-reduce | flops 2 | bytes 16 | tf_op jit(solution)/shard_map/psum | solution.py:40
  382.2 5.6 %all-reduce.3 = (f32[]{:T(128)}, f32[]{:T(128)}) all-reduce(f32[]{:T(128)} %get-tuple-element.7, f32[]{:T(128)} %get-tuple-element.8), channel_id=1, replica_groups=mesh['gx_0'=4,'gx_1'=2,'gy'=4,'gz_0'=2,'gz_1'=4] {'gz_0'}, use_global_device_ids=true, to_apply=%region_4.0 | all-reduce | flops 2 | bytes 16 | tf_op jit(solution)/shard_map/psum | solution.py:40
  387.9 9.4 %all-reduce = (f32[]{:T(128)}, f32[]{:T(128)}) all-reduce(f32[]{:T(128)} %get-tuple-element.11, f32[]{:T(128)} %get-tuple-element.12), channel_id=1, replica_groups=mesh['gx_0'=4,'gx_1'=2,'gy'=4,'gz_0'=2,'gz_1'=4] {'gz_1'}, use_global_device_ids=true, to_apply=%region_5.0 | all-reduce | flops 2 | bytes 16 | tf_op jit(solution)/shard_map/psum | solution.py:40
  398.5 3.4 copy.56
  401.9 5.1 %fusion.6 = f32[32,128,128]{2,1,0:T(8,128)} fusion(f32[32,8,16,128]{3,2,1,0:T(8,128)} %copy.56, f32[32,1,128,128]{3,2,1,0:T(8,128)} %all-to-all-done.5, f32[32,128,128]{2,1,0:T(8,128)} %param.4, f32[32,128,128]{2,1,0:T(8,128)S(1)} %copy-done.2, f32[]{:T(128)S(6)} %div.7, f32[]{:T(128)S(6)} %mul_shard_map.3), kind=kLoop, calls=%fused_computation.11 | loop fusion | flops 2621440 | bytes 10485768 | tf_op jit(solution)/shard_map/add | solution.py:80
  (24 shorter events, 31.0 us)
Async XLA Ops:
  0.0 115.2 %copy-start = (f32[512,512]{1,0:T(8,128)S(1)}, f32[512,512]{1,0:T(8,128)}, u32[]{:S(2)}) copy-start(f32[512,512]{1,0:T(8,128)} %param.6) | copy-start | bytes 3145732
  34.3 54.3 %all-to-all-start = ((f32[32,1,128,128]{3,2,1,0:T(8,128)}), f32[32,1,128,128]{3,2,1,0:T(8,128)S(1)}, u32[]{:S(2)}, u32[]{:S(2)}) async-start(f32[32,1,128,128]{3,2,1,0:T(8,128)} %bitcast), calls=%async_computation | async-start | bytes 4194304 | tf_op jit(solution)/shard_map/all_to_all | solution.py:33
  49.9 3.0 copy-start.3
  88.6 39.9 %all-to-all-start.3 = ((f32[256,16,128]{2,1,0:T(8,128)}), f32[256,16,128]{2,1,0:T(8,128)}, u32[]{:S(2)}, u32[]{:S(2)}) async-start(f32[256,16,128]{2,1,0:T(8,128)} %copy.47), calls=%async_computation.3 | async-start | bytes 4194304 | tf_op jit(solution)/shard_map/all_to_all | solution.py:66
  128.5 56.7 %all-to-all-start.1 = ((f32[32,1,128,128]{3,2,1,0:T(8,128)}), f32[32,1,128,128]{3,2,1,0:T(8,128)S(1)}, u32[]{:S(2)}, u32[]{:S(2)}) async-start(f32[32,1,128,128]{3,2,1,0:T(8,128)} %bitcast.114), calls=%async_computation.1 | async-start | bytes 4194304 | tf_op jit(solution)/shard_map/all_to_all | solution.py:33
  187.9 1.3 copy-start.1
  191.8 29.8 %all-to-all-start.6 = ((f32[32,128,128]{2,0,1:T(8,128)}), f32[32,128,128]{2,0,1:T(8,128)}, u32[]{:S(2)}, u32[]{:S(2)}) async-start(f32[32,128,128]{2,0,1:T(8,128)} %copy.53), calls=%async_computation.6 | async-start | bytes 4194304 | tf_op jit(solution)/shard_map/all_to_all | solution.py:70
  221.6 56.7 %all-to-all-start.4 = ((f32[32,1,128,128]{3,2,1,0:T(8,128)}), f32[32,1,128,128]{3,2,1,0:T(8,128)S(1)}, u32[]{:S(2)}, u32[]{:S(2)}) async-start(f32[32,1,128,128]{3,2,1,0:T(8,128)} %add.44), calls=%async_computation.4 | async-start | bytes 4194304 | tf_op jit(solution)/shard_map/all_to_all | solution.py:33
  278.3 29.8 %all-to-all-start.7 = ((f32[256,16,128]{2,1,0:T(8,128)}), f32[256,16,128]{2,1,0:T(8,128)}, u32[]{:S(2)}, u32[]{:S(2)}) async-start(f32[256,16,128]{2,1,0:T(8,128)} %copy.55), calls=%async_computation.7 | async-start | bytes 4194304 | tf_op jit(solution)/shard_map/all_to_all | solution.py:66
  308.1 93.8 %all-to-all-start.5 = ((f32[32,1,128,128]{3,2,1,0:T(8,128)}), f32[32,1,128,128]{3,2,1,0:T(8,128)}, u32[]{:S(2)}, u32[]{:S(2)}) async-start(f32[32,1,128,128]{3,2,1,0:T(8,128)} %bitcast.30), calls=%async_computation.5 | async-start | bytes 4194304 | tf_op jit(solution)/shard_map/all_to_all | solution.py:33
  398.5 3.4 copy-start.2
where the time goes:
time: 408 us; the launch traced here: 407 us
  waiting for transfers between devices  156 us (38%)
  blocking collectives  113 us (28%)
  starting transfers between devices  48.4 us (12%)
  local copies, waits for them, and re-layouts  41 us (10%)
  matrix products  33.8 us (8%)
  other arithmetic  13.7 us (3%)
    all_to_all x4, waiting for transfers between devices, joined_exchange(): tiles = lax.all_to_all(tiles, axis, split_axis=0, concat_axis=0, tiled=True)  119 us
    psum x5, blocking collectives, over_axes(): value = lax.psum(value, axis)  81.4 us
    all_to_all x1, blocking collectives, apply_block(): lax.all_to_all(tensor, GZ, split_axis=1, concat_axis=0, tiled=True)  31.4 us
    all_to_all x4, starting transfers between devices, joined_exchange(): tiles = lax.all_to_all(tiles, axis, split_axis=0, concat_axis=0, tiled=True)  25.7 us
    all_to_all x1, waiting for transfers between devices, apply_block(): lax.all_to_all(tensor, GZ, split_axis=1, concat_axis=0, tiled=True)  22.3 us
    all_to_all x2, starting transfers between devices, fibre_product(): return lax.all_to_all(product, GZ, split_axis=0, concat_axis=1, tiled=True)  18.4 us
    dot_general x2, matrix products, slab_products(): along_one = jnp.einsum('ip,mpj->mij', factor_a, slabs, precision=highest)  18.1 us
    all_to_all x2, waiting for transfers between devices, fibre_product(): return lax.all_to_all(product, GZ, split_axis=0, concat_axis=1, tiled=True)  14.6 us
  transfers between devices with their start and end apart: 7, of which 6 were waited for; matrix products, arithmetic and copies ran while one was open for 18% of the time, Pallas kernels for 0%

commit v1 on v0

--- a/solution.py
+++ b/solution.py
@@ -37,7 +37,7 @@
 
 def over_axes(value, axes):
     for axis in axes:
-        value = lax.psum(value, axis)
+        value = jnp.sum(lax.all_gather(value, axis), axis=0)
     return value
 
 

time: 408 us -> 430 us (1.054); the launches traced: 407 us -> 423 us
  local copies, waits for them, and re-layouts: 41 us -> 57.1 us
  blocking collectives: 113 us -> 106 us
  other arithmetic: 13.7 us -> 20.1 us
    psum x5 -> x0, blocking collectives: 81.4 us -> none  [over_axes(): value = lax.psum(value, axis)]
    unnamed x0 -> x5, blocking collectives: none -> 74.2 us
    unnamed x12 -> x47, local copies, waits for them, and re-layouts: 7.37 us -> 23.5 us
    reduce_sum x0 -> x10, other arithmetic: none -> 6.39 us  [over_axes(): value = jnp.sum(lax.all_gather(value, axis), axis=0)]
  transfers between devices with their start and end apart: 7 -> 7, of which waited for: 6 -> 6; matrix products, arithmetic and copies ran while one was open for 18% -> 23% of each run, Pallas kernels for 0% -> 0%
where the time goes in v1:
time: 430 us; the launch traced here: 423 us
  waiting for transfers between devices  156 us (36%)
  blocking collectives  106 us (25%)
  local copies, waits for them, and re-layouts  57.1 us (13%)
  starting transfers between devices  48.7 us (11%)
  matrix products  33.8 us (8%)
  other arithmetic  20.1 us (5%)
    all_to_all x4, waiting for transfers between devices, joined_exchange(): tiles = lax.all_to_all(tiles, axis, split_axis=0, concat_axis=0, tiled=True)  119 us
    unnamed x5, blocking collectives  74.2 us
    all_to_all x1, blocking collectives, apply_block(): lax.all_to_all(tensor, GZ, split_axis=1, concat_axis=0, tiled=True)  31.4 us
    all_to_all x4, starting transfers between devices, joined_exchange(): tiles = lax.all_to_all(tiles, axis, split_axis=0, concat_axis=0, tiled=True)  25.8 us
    unnamed x47, local copies, waits for them, and re-layouts  23.5 us
    all_to_all x1, waiting for transfers between devices, apply_block(): lax.all_to_all(tensor, GZ, split_axis=1, concat_axis=0, tiled=True)  22.2 us
    all_to_all x2, starting transfers between devices, fibre_product(): return lax.all_to_all(product, GZ, split_axis=0, concat_axis=1, tiled=True)  18.7 us
    dot_general x2, matrix products, slab_products(): along_one = jnp.einsum('ip,mpj->mij', factor_a, slabs, precision=highest)  18.1 us
  transfers between devices with their start and end apart: 7, of which 6 were waited for; matrix products, arithmetic and copies ran while one was open for 23% of the time, Pallas kernels for 0%

profile of v1, /device:TPU:32, one launch (start us, length us, event | category | flops | bytes accessed | tf_op | source)
XLA Modules:
  0.0 423.0 jit_solution(13523386483845049515)
XLA Ops:
  0.0 2.9 copy.44
  2.9 31.4 %all_to_all.89 = f32[32,128,128]{2,0,1:T(8,128)} all-to-all(f32[32,128,128]{2,0,1:T(8,128)S(1)} %copy.44), channel_id=1, replica_groups=mesh['gx_0'=4,'gx_1'=2,'gy'=4,'gz_0'=2,'gz_1'=4] {'gz_0','gz_1'}, dimensions={1} | all-to-all | bytes 4194304 | tf_op jit(solution)/shard_map/all_to_all | solution.py:70
  34.3 10.6 %all-to-all-start = ((f32[32,1,128,128]{3,2,1,0:T(8,128)}), f32[32,1,128,128]{3,2,1,0:T(8,128)S(1)}, u32[]{:S(2)}, u32[]{:S(2)}) async-start(f32[32,1,128,128]{3,2,1,0:T(8,128)} %bitcast.10), calls=%async_computation | async-start | bytes 4194304 | tf_op jit(solution)/shard_map/all_to_all | solution.py:33
  44.9 2.8 copy.45
  49.9 3.0 copy.46
  52.9 3.5 fusion.7
  59.0 29.6 %all-to-all-done = f32[32,1,128,128]{3,2,1,0:T(8,128)S(1)} async-done(((f32[32,1,128,128]{3,2,1,0:T(8,128)}), f32[32,1,128,128]{3,2,1,0:T(8,128)S(1)}, u32[]{:S(2)}, u32[]{:S(2)}) %all-to-all-start) | async-done | bytes 2097184 | tf_op jit(solution)/shard_map/all_to_all | solution.py:33
  88.6 14.4 %all-to-all-start.3 = ((f32[256,16,128]{2,1,0:T(8,128)}), f32[256,16,128]{2,1,0:T(8,128)}, u32[]{:S(2)}, u32[]{:S(2)}) async-start(f32[256,16,128]{2,1,0:T(8,128)} %copy.47), calls=%async_computation.3 | async-start | bytes 4194304 | tf_op jit(solution)/shard_map/all_to_all | solution.py:66
  106.4 9.1 %fusion.9 = f32[512,1024]{1,0:T(8,128)S(1)} fusion(f32[1024,512]{0,1:T(8,128)S(1)} %bitcast.123, f32[1024,1024]{1,0:T(8,128)} %param.5), kind=kOutput, calls=%fused_computation.16 | convolution fusion | flops 6442450944 | bytes 8388608 | tf_op jit(solution)/shard_map/ip,mpj->mij/dot_general | solution.py:50
  115.4 3.5 fusion.4
  121.3 7.4 %all-to-all-done.3 = f32[256,16,128]{2,1,0:T(8,128)} async-done(((f32[256,16,128]{2,1,0:T(8,128)}), f32[256,16,128]{2,1,0:T(8,128)}, u32[]{:S(2)}, u32[]{:S(2)}) %all-to-all-start.3) | async-done | bytes 2097184 | tf_op jit(solution)/shard_map/all_to_all | solution.py:66
  128.7 5.0 %all-to-all-start.1 = ((f32[32,1,128,128]{3,2,1,0:T(8,128)}), f32[32,1,128,128]{3,2,1,0:T(8,128)S(1)}, u32[]{:S(2)}, u32[]{:S(2)}) async-start(f32[32,1,128,128]{3,2,1,0:T(8,128)} %bitcast.129), calls=%async_computation.1 | async-start | bytes 4194304 | tf_op jit(solution)/shard_map/all_to_all | solution.py:33
  133.7 3.2 copy.48
  136.9 48.5 %all-to-all-done.1 = f32[32,1,128,128]{3,2,1,0:T(8,128)S(1)} async-done(((f32[32,1,128,128]{3,2,1,0:T(8,128)}), f32[32,1,128,128]{3,2,1,0:T(8,128)S(1)}, u32[]{:S(2)}, u32[]{:S(2)}) %all-to-all-start.1) | async-done | bytes 2097184 | tf_op jit(solution)/shard_map/all_to_all | solution.py:33
  192.0 4.3 %all-to-all-start.6 = ((f32[32,128,128]{2,0,1:T(8,128)}), f32[32,128,128]{2,0,1:T(8,128)}, u32[]{:S(2)}, u32[]{:S(2)}) async-start(f32[32,128,128]{2,0,1:T(8,128)} %copy.53), calls=%async_computation.6 | async-start | bytes 4194304 | tf_op jit(solution)/shard_map/all_to_all | solution.py:70
  196.4 3.1 add.24
  199.5 22.2 %all-to-all-done.6 = f32[32,128,128]{2,0,1:T(8,128)} async-done(((f32[32,128,128]{2,0,1:T(8,128)}), f32[32,128,128]{2,0,1:T(8,128)}, u32[]{:S(2)}, u32[]{:S(2)}) %all-to-all-start.6) | async-done | bytes 2097184 | tf_op jit(solution)/shard_map/all_to_all | solution.py:70
  221.7 5.1 %all-to-all-start.4 = ((f32[32,1,128,128]{3,2,1,0:T(8,128)}), f32[32,1,128,128]{3,2,1,0:T(8,128)S(1)}, u32[]{:S(2)}, u32[]{:S(2)}) async-start(f32[32,1,128,128]{3,2,1,0:T(8,128)} %add.24), calls=%async_computation.4 | async-start | bytes 4194304 | tf_op jit(solution)/shard_map/all_to_all | solution.py:33
  229.7 5.0 %fusion = f32[2048,256]{1,0:T(8,128)} fusion(f32[256,256]{1,0:T(8,128)S(1)} %copy-done.3, f32[32,8,16,128]{3,2,1,0:T(8,128)S(1)} %bitcast.136), kind=kOutput, calls=%fused_computation | convolution fusion | flops 1610612736 | bytes 4456448 | tf_op jit(solution)/shard_map/dot_general | solution.py:65
  234.7 3.0 copy.55
  237.7 40.9 %all-to-all-done.4 = f32[32,1,128,128]{3,2,1,0:T(8,128)S(1)} async-done(((f32[32,1,128,128]{3,2,1,0:T(8,128)}), f32[32,1,128,128]{3,2,1,0:T(8,128)S(1)}, u32[]{:S(2)}, u32[]{:S(2)}) %all-to-all-start.4) | async-done | bytes 2097184 | tf_op jit(solution)/shard_map/all_to_all | solution.py:33
  278.6 4.3 %all-to-all-start.7 = ((f32[256,16,128]{2,1,0:T(8,128)}), f32[256,16,128]{2,1,0:T(8,128)}, u32[]{:S(2)}, u32[]{:S(2)}) async-start(f32[256,16,128]{2,1,0:T(8,128)} %copy.55), calls=%async_computation.7 | async-start | bytes 4194304 | tf_op jit(solution)/shard_map/all_to_all | solution.py:66
  286.3 9.1 %fusion.10 = f32[512,1024]{1,0:T(8,128)S(1)} fusion(f32[1024,512]{0,1:T(8,128)S(1)} %bitcast.125, f32[1024,1024]{1,0:T(8,128)} %param.5), kind=kOutput, calls=%fused_computation.17 | convolution fusion | flops 6442450944 | bytes 8388608 | tf_op jit(solution)/shard_map/ip,mpj->mij/dot_general | solution.py:50
  295.4 3.5 fusion.3
  301.3 7.2 %all-to-all-done.7 = f32[256,16,128]{2,1,0:T(8,128)} async-done(((f32[256,16,128]{2,1,0:T(8,128)}), f32[256,16,128]{2,1,0:T(8,128)}, u32[]{:S(2)}, u32[]{:S(2)}) %all-to-all-start.7) | async-done | bytes 2097184 | tf_op jit(solution)/shard_map/all_to_all | solution.py:66
  308.4 5.1 %all-to-all-start.5 = ((f32[32,1,128,128]{3,2,1,0:T(8,128)}), f32[32,1,128,128]{3,2,1,0:T(8,128)}, u32[]{:S(2)}, u32[]{:S(2)}) async-start(f32[32,1,128,128]{3,2,1,0:T(8,128)} %bitcast.45), calls=%async_computation.5 | async-start | bytes 4194304 | tf_op jit(solution)/shard_map/all_to_all | solution.py:33
  320.1 47.9 %all-reduce.12 = (f32[4]{0:T(128)S(1)}, f32[4]{0:T(128)S(1)}) all-reduce(f32[4]{0:T(128)S(1)} %dynamic-update-slice, f32[4]{0:T(128)S(1)} %dynamic-update-slice.5), channel_id=1, replica_groups=mesh['gx_0'=4,'gx_1'=2,'gy'=4,'gz_0'=2,'gz_1'=4] {'gx_0'}, use_global_device_ids=true, to_apply=%add | all-reduce | flops 8 | bytes 64
  379.5 10.2 %all-reduce.11 = (f32[4]{0:T(128)S(1)}, f32[4]{0:T(128)S(1)}) all-reduce(f32[4]{0:T(128)S(1)} %dynamic-update-slice.2, f32[4]{0:T(128)S(1)} %dynamic-update-slice.7), channel_id=1, replica_groups=mesh['gx_0'=4,'gx_1'=2,'gy'=4,'gz_0'=2,'gz_1'=4] {'gy'}, use_global_device_ids=true, to_apply=%add.2 | all-reduce | flops 8 | bytes 64
  394.3 4.9 %all-reduce.13 = (f32[2]{0:T(128)S(1)}, f32[2]{0:T(128)S(1)}) all-reduce(f32[2]{0:T(128)S(1)} %dynamic-update-slice.3, f32[2]{0:T(128)S(1)} %dynamic-update-slice.8), channel_id=1, replica_groups=mesh['gx_0'=4,'gx_1'=2,'gy'=4,'gz_0'=2,'gz_1'=4] {'gz_0'}, use_global_device_ids=true, to_apply=%add.3 | all-reduce | flops 4 | bytes 32
  403.1 8.7 %all-reduce.10 = (f32[4]{0:T(128)S(1)}, f32[4]{0:T(128)S(1)}) all-reduce(f32[4]{0:T(128)S(1)} %dynamic-update-slice.4, f32[4]{0:T(128)S(1)} %dynamic-update-slice.9), channel_id=1, replica_groups=mesh['gx_0'=4,'gx_1'=2,'gy'=4,'gz_0'=2,'gz_1'=4] {'gz_1'}, use_global_device_ids=true, to_apply=%add.4 | all-reduce | flops 8 | bytes 64
  414.2 3.4 copy.56
  417.6 5.1 %fusion.6 = f32[32,128,128]{2,1,0:T(8,128)} fusion(f32[32,8,16,128]{3,2,1,0:T(8,128)} %copy.56, f32[32,1,128,128]{3,2,1,0:T(8,128)} %all-to-all-done.5, f32[32,128,128]{2,1,0:T(8,128)} %param.4, f32[32,128,128]{2,1,0:T(8,128)S(1)} %copy-done.2, f32[]{:T(128)S(6)} %div.7, f32[]{:T(128)S(6)} %mul_shard_map.3), kind=kLoop, calls=%fused_computation.11 | loop fusion | flops 2621440 | bytes 10485768 | tf_op jit(solution)/shard_map/add | solution.py:80
  (69 shorter events, 53.2 us)
Async XLA Ops:
  0.0 115.4 %copy-start = (f32[512,512]{1,0:T(8,128)S(1)}, f32[512,512]{1,0:T(8,128)}, u32[]{:S(2)}) copy-start(f32[512,512]{1,0:T(8,128)} %param.6) | copy-start | bytes 3145732
  34.3 54.3 %all-to-all-start = ((f32[32,1,128,128]{3,2,1,0:T(8,128)}), f32[32,1,128,128]{3,2,1,0:T(8,128)S(1)}, u32[]{:S(2)}, u32[]{:S(2)}) async-start(f32[32,1,128,128]{3,2,1,0:T(8,128)} %bitcast.10), calls=%async_computation | async-start | bytes 4194304 | tf_op jit(solution)/shard_map/all_to_all | solution.py:33
  49.9 3.0 copy-start.3
  88.6 40.1 %all-to-all-start.3 = ((f32[256,16,128]{2,1,0:T(8,128)}), f32[256,16,128]{2,1,0:T(8,128)}, u32[]{:S(2)}, u32[]{:S(2)}) async-start(f32[256,16,128]{2,1,0:T(8,128)} %copy.47), calls=%async_computation.3 | async-start | bytes 4194304 | tf_op jit(solution)/shard_map/all_to_all | solution.py:66
  128.7 56.7 %all-to-all-start.1 = ((f32[32,1,128,128]{3,2,1,0:T(8,128)}), f32[32,1,128,128]{3,2,1,0:T(8,128)S(1)}, u32[]{:S(2)}, u32[]{:S(2)}) async-start(f32[32,1,128,128]{3,2,1,0:T(8,128)} %bitcast.129), calls=%async_computation.1 | async-start | bytes 4194304 | tf_op jit(solution)/shard_map/all_to_all | solution.py:33
  188.1 1.4 copy-start.1
  192.0 29.7 %all-to-all-start.6 = ((f32[32,128,128]{2,0,1:T(8,128)}), f32[32,128,128]{2,0,1:T(8,128)}, u32[]{:S(2)}, u32[]{:S(2)}) async-start(f32[32,128,128]{2,0,1:T(8,128)} %copy.53), calls=%async_computation.6 | async-start | bytes 4194304 | tf_op jit(solution)/shard_map/all_to_all | solution.py:70
  221.7 56.9 %all-to-all-start.4 = ((f32[32,1,128,128]{3,2,1,0:T(8,128)}), f32[32,1,128,128]{3,2,1,0:T(8,128)S(1)}, u32[]{:S(2)}, u32[]{:S(2)}) async-start(f32[32,1,128,128]{3,2,1,0:T(8,128)} %add.24), calls=%async_computation.4 | async-start | bytes 4194304 | tf_op jit(solution)/shard_map/all_to_all | solution.py:33
  278.6 29.8 %all-to-all-start.7 = ((f32[256,16,128]{2,1,0:T(8,128)}), f32[256,16,128]{2,1,0:T(8,128)}, u32[]{:S(2)}, u32[]{:S(2)}) async-start(f32[256,16,128]{2,1,0:T(8,128)} %copy.55), calls=%async_computation.7 | async-start | bytes 4194304 | tf_op jit(solution)/shard_map/all_to_all | solution.py:66
  308.4 5.1 %copy-start.8 = (u32[256]{0:T(256)S(1)}, u32[256]{0:T(256)}, u32[]{:S(2)}) copy-start(u32[256]{0:T(256)} %constant.13) | copy-start | bytes 3076
  308.4 109.2 %all-to-all-start.5 = ((f32[32,1,128,128]{3,2,1,0:T(8,128)}), f32[32,1,128,128]{3,2,1,0:T(8,128)}, u32[]{:S(2)}, u32[]{:S(2)}) async-start(f32[32,1,128,128]{3,2,1,0:T(8,128)} %bitcast.45), calls=%async_computation.5 | async-start | bytes 4194304 | tf_op jit(solution)/shard_map/all_to_all | solution.py:33
  313.5 6.0 %copy-start.7 = (u32[256]{0:T(256)S(1)}, u32[256]{0:T(256)}, u32[]{:S(2)}) copy-start(u32[256]{0:T(256)} %constant.18) | copy-start | bytes 3076
  313.5 58.4 %copy-start.6 = (u32[256]{0:T(256)S(1)}, u32[256]{0:T(256)}, u32[]{:S(2)}) copy-start(u32[256]{0:T(256)} %constant.23) | copy-start | bytes 3076
  313.5 65.4 %copy-start.5 = (u32[256]{0:T(256)S(1)}, u32[256]{0:T(256)}, u32[]{:S(2)}) copy-start(u32[256]{0:T(256)} %constant.28) | copy-start | bytes 3076
  313.6 80.1 %copy-start.4 = (u32[256]{0:T(256)S(1)}, u32[256]{0:T(256)}, u32[]{:S(2)}) copy-start(u32[256]{0:T(256)} %constant.33) | copy-start | bytes 3076
  414.2 3.4 copy-start.2
